TPU v7x, 32 devices: a whole 2x2x4 slice. The times are simulated.
32 devices in a mesh: vocab: 16 (over z, x, core), seq: 2 (over y).
Axes of the slice: x: 2, y: 2, z: 4, core: 2. Of those that a mesh axis runs over, the one named last changes fastest.
Arguments:
- hidden_states: bfloat16 [512, 3584], P('seq', 'vocab'), may hold values from -6 to 6
- norm_gain: float32 [3584], replicated, may hold values from 0.5 to 1.5
- embedding: bfloat16 [256000, 3584], P(('vocab', 'seq')), may hold values from -0.29882812 to 0.29882812
- targets: int32 [512], replicated, may hold values from 0 to 255999
Outputs:
- token_loss: float32 [512], P('seq')
- mean_loss: float32 [], replicated
All inputs are finite; a program needn't handle non-finite values.
Results may differ from a plain program's by a relative error of at most 0.0005.
Values may be sent and summed in bfloat16 or wider, within the bound.
A program may use at most 128 MiB of HBM per device.

v0:
```python
import functools

import jax
import jax.numpy as jnp
from jax import lax
from jax.experimental import pallas as pl
from jax.experimental.pallas import tpu as pltpu
from jax.sharding import PartitionSpec as P

LANES = 128
SLOTS = 3
LOG2E = 1.4426950408889634


def tile_rows(rows, limit):
    best = rows
    for unit in (16, 8):
        sizes = [n for n in range(unit, limit + 1, unit) if rows % n == 0]
        if sizes:
            return max(sizes)
    return best


def kernel(cfg, ht_ref, gain_ref, targets_ref, emb_ref, loss_ref, mean_ref,
           raw, normed, acc, buf_a, buf_b, gcol, stat, rbuf, fin, lossbuf, sums,
           z_send, z_recv, p_send, p_recv, c_send, c_recv, s_send, s_recv,
           f_send, f_recv, own_sem, a_sem, b_sem):
    nv, ns, group, planes, width, own, tokens, rows, tm, features, sub = cfg
    v, s = lax.axis_index("vocab"), lax.axis_index("seq")
    p, q = v // group, v % group
    core = q % 2
    half = (group // 2) * ns
    hidx = (q // 2) * ns + s
    count = nv * ns
    me = s * nv + v
    gw = group * width
    tiles = rows // tm

    def plane_of(k):
        return (p + k) % planes

    def remote(src, dst, send, recv, vv, ss):
        return pltpu.make_async_remote_copy(
            src_ref=src, dst_ref=dst, send_sem=send, recv_sem=recv,
            device_id={"vocab": vv, "seq": ss},
            device_id_type=pl.DeviceIdType.MESH)

    first = planes - 2

    def a_copy(k, i, slot):
        col = pl.multiple_of(plane_of(k) * gw, LANES)
        row = pl.multiple_of(i * tm, 8)
        return pltpu.make_async_copy(
            emb_ref.at[pl.ds(row, tm), pl.ds(col, gw)], buf_a.at[slot], a_sem.at[slot])

    def b_copy(i, slot, part):
        col = pl.multiple_of(plane_of(first + part) * gw, LANES)
        row = pl.multiple_of(i * tm, 8)
        return pltpu.make_async_copy(
            emb_ref.at[pl.ds(row, tm), pl.ds(col, gw)],
            buf_b.at[slot, :, pl.ds(part * gw, gw)], b_sem.at[slot, part])

    total_a = first * tiles

    def a_start(n):
        for k in range(first):
            @pl.when((n >= k * tiles) & (n < (k + 1) * tiles))
            def _():
                a_copy(k, n - k * tiles, n % SLOTS).start()

    for n in range(min(SLOTS - 1, total_a)):
        a_copy(n // tiles, n % tiles, n % SLOTS).start()
    for n in range(min(SLOTS - 1, tiles)):
        for part in range(2):
            b_copy(n, n, part).start()

    barrier = pltpu.get_barrier_semaphore()

    def greet(d, _):
        peer = (me + d) % count
        pl.semaphore_signal(barrier, inc=1,
                            device_id={"vocab": peer % nv, "seq": peer // nv},
                            device_id_type=pl.DeviceIdType.MESH)
        return 0

    lax.fori_loop(1, count, greet, 0)
    h = ht_ref[...].astype(jnp.float32)
    stat[me] = jnp.sum(h * h, axis=0, keepdims=True)

    for k in range(planes):
        for i in range(gw // LANES):
            row = plane_of(k) * (gw // LANES) + i
            gcol[k * gw + i * LANES:k * gw + (i + 1) * LANES, :] = jnp.broadcast_to(
                gain_ref[pl.ds(row, 1), :], (LANES, LANES)).T
    pl.semaphore_wait(barrier, count - 1)

    def tile_at(k, qq, ss):
        return raw.at[k, pl.ds(pl.multiple_of(qq * width, 16), width),
                      pl.ds(pl.multiple_of(ss * own, LANES), own)]

    def own_of(k):
        return ht_ref if k == 0 else tile_at(k, q, s)

    def z_copy(k):
        target = (p + planes - k) % planes
        return remote(ht_ref, tile_at(k, q, s), z_send.at[k], z_recv.at[k],
                      target * group + q, s)

    def p_copy(k, j):
        other = (hidx + j) % half
        return remote(own_of(k), tile_at(k, q, s), p_send.at[k, j], p_recv.at[k, j],
                      p * group + 2 * (other // ns) + core, other % ns)

    def c_copy(k, j):
        tile = (hidx + half - j) % half
        place = tile_at(k, 2 * (tile // ns) + core, tile % ns)
        return remote(place, place, c_send.at[k, j], c_recv.at[k, j],
                      p * group + (q + 1 - 2 * core), s)

    def c_own(k):
        return remote(own_of(k), tile_at(k, q, s), c_send.at[k, 0], c_recv.at[k, 0],
                      p * group + (q + 1 - 2 * core), s)

    def s_copy(d):
        peer = (me + d) % count
        return remote(stat.at[me], stat.at[me], s_send.at[d], s_recv.at[d],
                      peer % nv, peer // nv)

    def loop(low, high, action):
        def body(i, _):
            action(i)
            return 0
        lax.fori_loop(low, high, body, 0)

    def spread(k):
        loop(1, half, lambda j: p_copy(k, j).start())
        c_own(k).start()

    def relay(k):
        def one(j):
            p_copy(k, j).wait_recv()
            c_copy(k, j).start()
        loop(1, half, one)

    loop(1, count, lambda d: s_copy(d).start())
    spread(0)
    for k in range(1, planes):
        z_copy(k).start()
    own_copy = pltpu.make_async_copy(ht_ref, tile_at(0, q, s), own_sem)
    own_copy.start()

    loop(1, count, lambda d: s_copy(d).wait_recv())
    for t in range(ns):
        part = stat[t * nv:(t + 1) * nv]
        meansq = jnp.sum(part, axis=0) / features
        rbuf[:, t * own:(t + 1) * own] = lax.rsqrt(meansq + 1e-06)

    relay(0)

    def normalize(k):
        loop(0, half, lambda j: c_copy(k, j).wait_recv())
        for i in range(gw // LANES):
            gain = gcol[k * gw + i * LANES:k * gw + (i + 1) * LANES, :]
            for c in range(tokens // LANES):
                cols = slice(c * LANES, (c + 1) * LANES)
                values = raw[k, i * LANES:(i + 1) * LANES, cols].astype(jnp.float32)
                out = values * rbuf[:, cols] * gain
                normed[k * gw + i * LANES:k * gw + (i + 1) * LANES, cols] = (
                    out.astype(jnp.bfloat16))

    own_copy.wait()
    normalize(0)

    def step_a(k, i):
        n = k * tiles + i
        a_copy(k, i, n % SLOTS).wait()

        @pl.when(n + SLOTS - 1 < total_a)
        def _():
            a_start(n + SLOTS - 1)

        place = pl.ds(pl.multiple_of(i * tm, 8), tm)
        product = jnp.dot(buf_a[n % SLOTS], normed[k * gw:(k + 1) * gw, :],
                          preferred_element_type=jnp.float32)
        if k == 0:
            acc[place, :] = product
        else:
            acc[place, :] += product

    base = (v * ns + s) * rows

    def step_b(i):
        slot = i % SLOTS
        for part in range(2):
            b_copy(i, slot, part).wait()

        @pl.when(i + SLOTS - 1 < tiles)
        def _():
            for part in range(2):
                b_copy(i + SLOTS - 1, (i + SLOTS - 1) % SLOTS, part).start()

        total = sums[0:8, :]
        picked = sums[8:16, :]
        for m in range(tm // sub):
            place = pl.ds(pl.multiple_of(i * tm + m * sub, 8), sub)
            scores = jnp.dot(buf_b[slot, m * sub:(m + 1) * sub, :],
                             normed[first * gw:planes * gw, :],
                             preferred_element_type=jnp.float32)
            if first > 0:
                scores = scores + acc[place, :]
            bent = jnp.tanh(scores * (1.0 / 30.0))
            grown = jnp.exp2(bent * (30.0 * LOG2E))
            want = targets_ref[...] - (base + i * tm + m * sub)
            hit = lax.broadcasted_iota(jnp.int32, (sub, tokens), 0) == want
            mine = jnp.where(hit, bent, 0.0)
            total = total + jnp.sum(grown.reshape(sub // 8, 8, tokens), axis=0)
            picked = picked + jnp.sum(mine.reshape(sub // 8, 8, tokens), axis=0)
        sums[0:8, :] = total
        sums[8:16, :] = picked

    def ready(k):
        z_copy(k).wait_recv()
        spread(k)

    sums[...] = jnp.zeros_like(sums)
    ready(1)
    for k in range(first):
        nexts = [k + 1] if k + 1 < first else [k + 1, k + 2]
        events = []
        if k == 0:
            events += [((e - 1) * tiles // planes, ready, e) for e in range(2, planes)]
        marks = (6,) if len(nexts) == 1 else (4, 9)
        events += [(mark * tiles // 10, relay, e) for mark, e in zip(marks, nexts)]
        done = 0
        for at, action, e in sorted(events, key=lambda event: event[0]):
            if at > done:
                loop(done, at, functools.partial(step_a, k))
                done = at
            action(e)
        loop(done, tiles, functools.partial(step_a, k))
        for e in nexts:
            normalize(e)
    loop(0, tiles, step_b)

    def f_copy(d):
        peer = (me + d) % count
        return remote(fin.at[me], fin.at[me], f_send.at[d], f_recv.at[d],
                      peer % nv, peer // nv)

    fin[me, 0:1, :] = jnp.sum(sums[0:8, :], axis=0, keepdims=True)
    fin[me, 1:2, :] = jnp.sum(sums[8:16, :], axis=0, keepdims=True)
    loop(1, count, lambda d: f_copy(d).start())
    loop(1, count, lambda d: f_copy(d).wait_recv())
    both = jnp.sum(fin[...], axis=0)
    losses = jnp.log(both[0:1, :]) - 30.0 * both[1:2, :]
    lossbuf[...] = losses
    mean_ref[...] = jnp.sum(losses, axis=1, keepdims=True) / tokens
    loss_ref[...] = lossbuf[:, pl.ds(pl.multiple_of(s * own, LANES), own)]

    loop(1, count, lambda d: s_copy(d).wait_send())
    for k in range(planes):
        if k > 0:
            z_copy(k).wait_send()
        loop(1, half, lambda j: p_copy(k, j).wait_send())
        loop(0, half, lambda j: c_copy(k, j).wait_send())
    loop(1, count, lambda d: f_copy(d).wait_send())


def local(nv, ns, hidden_states, norm_gain, embedding, targets):
    own, width = hidden_states.shape
    rows, features = embedding.shape
    tokens = targets.shape[0]
    group = 2
    while (group * width) % LANES:
        group *= 2
    planes = nv // group
    gw = group * width
    tm = tile_rows(rows, 800)
    sub = tile_rows(tm, 200)
    half = (group // 2) * ns
    count = nv * ns
    cfg = (nv, ns, group, planes, width, own, tokens, rows, tm, features, sub)
    dma = pltpu.SemaphoreType.DMA
    vmem = pl.BlockSpec(memory_space=pltpu.VMEM)
    loss, mean = pl.pallas_call(
        functools.partial(kernel, cfg),
        out_shape=(jax.ShapeDtypeStruct((1, own), jnp.float32),
                   jax.ShapeDtypeStruct((1, 1), jnp.float32)),
        in_specs=[vmem, vmem, vmem, pl.BlockSpec(memory_space=pl.ANY)],
        out_specs=(vmem, vmem),
        scratch_shapes=[
            pltpu.VMEM((planes, gw, tokens), jnp.bfloat16),
            pltpu.VMEM((features, tokens), jnp.bfloat16),
            pltpu.VMEM((rows, tokens), jnp.float32),
            pltpu.VMEM((SLOTS, tm, gw), jnp.bfloat16),
            pltpu.VMEM((SLOTS, tm, 2 * gw), jnp.bfloat16),
            pltpu.VMEM((features, LANES), jnp.float32),
            pltpu.VMEM((count, 1, own), jnp.float32),
            pltpu.VMEM((1, tokens), jnp.float32),
            pltpu.VMEM((count, 2, tokens), jnp.float32),
            pltpu.VMEM((1, tokens), jnp.float32),
            pltpu.VMEM((16, tokens), jnp.float32),
            dma((planes,)), dma((planes,)),
            dma((planes, half)), dma((planes, half)),
            dma((planes, half)), dma((planes, half)),
            dma((count,)), dma((count,)),
            dma((count,)), dma((count,)),
            dma, dma((SLOTS,)), dma((SLOTS, 2)),
        ],
        compiler_params=pltpu.CompilerParams(
            collective_id=0, has_side_effects=True, vmem_limit_bytes=60 * 2**20),
    )(hidden_states.T, norm_gain.reshape(-1, LANES), targets.reshape(1, -1), embedding)
    return loss.reshape(own), mean.reshape(())


def solution(mesh):
    placed = (P("seq", "vocab"), P(), P(("vocab", "seq"), None), P())
    body = functools.partial(local, mesh.shape["vocab"], mesh.shape["seq"])
    return jax.shard_map(
        body, mesh=mesh, in_specs=placed, out_specs=(P("seq"), P()), check_vma=False
    )
```

profile of v0, /device:TPU:0, one launch (start us, length us, event | category | flops | bytes accessed | tf_op | source)
XLA Modules:
  0.0 69.3 jit_solution(6697762820645984578)
XLA Ops:
  0.6 65.7 %shard_map.59 = (f32[1,256]{1,0:T(1,128)}, f32[1,1]{1,0:T(1,128)}) custom-call(bf16[224,256]{1,0:T(8,128)(2,1)} %bitcast.5, f32[28,128]{1,0:T(8,128)} %bitcast.6, s32[1,512]{1,0:T(1,128)} %bitcast.7, bf16[8000,3584]{1,0:T(8,128)(2,1)} %emb_ref.1), custom_call_target="tpu_custom_call" | custom-call | tf_op jit(solution)/shard_map/pallas_call | solution.py:285
  66.3 1.2 %copy.8 = f32[256]{0:T(256)} copy(f32[256]{0:T(256)} %bitcast.8) | data formatting | bytes 2048
where the time goes:
time: 69.5 us; the launch traced here: 69.3 us
  Pallas kernels  65.7 us (95%)
  between operations  2.4 us (3%)
  local copies, waits for them, and re-layouts  1.22 us (2%)
    pallas_call x1, Pallas kernels, local(): pl.pallas_call(functools.partial(kernel, cfg), out_shape=(jax.ShapeDtypeS...  65.7 us

commit v1 on v0

v1 whole, which is shorter than its diff:
```python
import functools

import jax
import jax.numpy as jnp
from jax import lax
from jax.experimental import pallas as pl
from jax.experimental.pallas import tpu as pltpu
from jax.sharding import PartitionSpec as P

LANES = 128
MXU = 256
UNROLL = 2
LOG2E = 1.4426950408889634


def block_rows(rows, limit):
    return max(n for n in range(16, limit + 1, 16) if rows % n == 0)


def cut_phases(planes, gw):
    ends = [(k + 1) * gw // MXU * MXU for k in range(planes)]
    ends[-1] = planes * gw
    return [(a, b - a) for a, b in zip([0] + ends[:-1], ends)]


def kernel(cfg, ht_ref, gain_ref, targets_ref, emb_ref, loss_ref, mean_ref,
           raw, zbuf, normed, acc, area_a, area_b, gcol, stat, rbuf, fin, lossbuf,
           sums, z_send, z_recv, p_send, p_recv, c_send, c_recv, s_send, s_recv,
           f_send, f_recv, own_sem, e_sem):
    nv, ns, group, planes, width, own, tokens, rows, padded, bm, features = cfg
    v, s = lax.axis_index("vocab"), lax.axis_index("seq")
    p, q = v // group, v % group
    core = q % 2
    half = (group // 2) * ns
    hidx = (q // 2) * ns + s
    count = nv * ns
    me = s * nv + v
    gw = group * width
    phases = cut_phases(planes, gw)
    nblk = padded // bm
    lanes_of = lambda i: pl.ds(pl.multiple_of(i * LANES, LANES), LANES)

    def plane_of(k):
        return (p + planes - k) % planes

    def loop(low, high, action):
        def body(i, _):
            action(i)
            return 0
        lax.fori_loop(low, high, body, 0)

    def area(ph):
        return area_a if ph % 2 == 0 else area_b

    def table_copies(ph):
        first, size = phases[ph]
        copies, at = [], first
        while at < first + size:
            k = at // gw
            end = min((k + 1) * gw, first + size)
            col = pl.multiple_of(plane_of(k) * gw + at % gw, LANES)
            copies.append(pltpu.make_async_copy(
                emb_ref.at[:, pl.ds(col, end - at)],
                area(ph).at[pl.ds(0, rows), pl.ds(at - first, end - at)],
                e_sem.at[ph, len(copies)]))
            at = end
        return copies

    def fetch(ph):
        for copy in table_copies(ph):
            copy.start()

    def fetched(ph):
        for copy in table_copies(ph):
            copy.wait()

    def peer_of(e):
        dp, rest = e // (group * ns), e % (group * ns)
        return (((p + planes - dp) % planes) * group + (q + rest // ns) % group,
                (s + rest % ns) % ns)

    barrier = pltpu.get_barrier_semaphore()

    def greet(e):
        vv, ss = peer_of(e)
        pl.semaphore_signal(barrier, inc=1, device_id={"vocab": vv, "seq": ss},
                            device_id_type=pl.DeviceIdType.MESH)

    loop(1, count, greet)
    fetch(0)
    if len(phases) > 1:
        fetch(1)
    h = ht_ref[...].astype(jnp.float32)
    stat[me] = jnp.sum(h * h, axis=0, keepdims=True)
    pl.semaphore_wait(barrier, count - 1)

    def remote(src, dst, send, recv, vv, ss):
        return pltpu.make_async_remote_copy(
            src_ref=src, dst_ref=dst, send_sem=send, recv_sem=recv,
            device_id={"vocab": vv, "seq": ss},
            device_id_type=pl.DeviceIdType.MESH)

    def tile_at(k, qq, ss):
        place = raw if k == 0 else normed
        row = 0 if k == 0 else k * gw
        return place.at[pl.ds(pl.multiple_of(row + qq * width, 16), width),
                        pl.ds(pl.multiple_of(ss * own, LANES), own)]

    def own_of(k):
        return ht_ref if k == 0 else tile_at(k, q, s)

    def z_copy(k):
        return remote(ht_ref, zbuf.at[k - 1], z_send.at[k], z_recv.at[k],
                      (p + k) % planes * group + q, s)

    def p_copy(k, j):
        other = (hidx + j) % half
        return remote(own_of(k), tile_at(k, q, s), p_send.at[k, j], p_recv.at[k, j],
                      p * group + 2 * (other // ns) + core, other % ns)

    def c_copy(k, j):
        tile = (hidx + half - j) % half
        place = tile_at(k, 2 * (tile // ns) + core, tile % ns)
        return remote(place, place, c_send.at[k, j], c_recv.at[k, j],
                      p * group + (q + 1 - 2 * core), s)

    def c_own(k):
        return remote(own_of(k), tile_at(k, q, s), c_send.at[k, 0], c_recv.at[k, 0],
                      p * group + (q + 1 - 2 * core), s)

    def s_copy(e):
        return remote(stat.at[me], stat.at[me], s_send.at[e], s_recv.at[e], *peer_of(e))

    def spread(k):
        loop(1, half, lambda j: p_copy(k, j).start())
        c_own(k).start()

    def relay(k):
        def one(j):
            p_copy(k, j).wait_recv()
            c_copy(k, j).start()
        loop(1, half, one)

    def gathered(k):
        loop(0, half, lambda j: c_copy(k, j).wait_recv())

    loop(1, count, lambda e: s_copy(e).start())
    spread(0)
    for k in range(1, planes):
        z_copy(k).start()
    own_copy = pltpu.make_async_copy(ht_ref, tile_at(0, q, s), own_sem)
    own_copy.start()

    for k in range(planes):
        for i in range(gw // LANES):
            row = plane_of(k) * (gw // LANES) + i
            gcol[k * gw + i * LANES:k * gw + (i + 1) * LANES, :] = jnp.broadcast_to(
                gain_ref[pl.ds(row, 1), :], (LANES, LANES)).T
    sums[...] = jnp.zeros_like(sums)
    if padded > rows:
        for area_ref in (area_a, area_b):
            area_ref[rows // 16 * 16:, :] = jnp.zeros(
                (padded - rows // 16 * 16, area_ref.shape[1]), jnp.bfloat16)

    relay(0)
    loop(1, count, lambda e: s_copy(e).wait_recv())
    for t in range(ns):
        meansq = jnp.sum(stat[t * nv:(t + 1) * nv], axis=0) / features
        rbuf[:, t * own:(t + 1) * own] = lax.rsqrt(meansq + 1e-06)

    def ready(k):
        z_copy(k).wait_recv()
        place = tile_at(k, q, s)
        for c in range(own // LANES):
            scale = rbuf[:, lanes_of(s * (own // LANES) + c)]
            values = zbuf[k - 1, :, c * LANES:(c + 1) * LANES].astype(jnp.float32)
            gain = gcol[pl.ds(pl.multiple_of(k * gw + q * width, 16), width), :]
            place[:, c * LANES:(c + 1) * LANES] = (values * scale * gain).astype(jnp.bfloat16)
        spread(k)

    def run(*held):
        cols_of = [list(range(c, min(c + 2, tokens // MXU))) for c in range(0, tokens // MXU, 2)]
        accs = [held[0:2], held[2:4]]

        def push(ph, cols, i, reg):
            at = phases[ph][0] + i * MXU
            for m, c in enumerate(cols):
                pltpu.matmul_push_rhs(
                    normed[at:at + MXU, c * MXU:(c + 1) * MXU],
                    staging_register=reg, mxu_index=m)

        def feed(ph, cols, block, turn, seq, more):
            passes = phases[ph][1] // MXU
            place = pl.ds(pl.multiple_of(block * bm, 16), bm)
            for i in range(passes):
                reg = (seq + i) % 2
                part = area(ph)[place, i * MXU:(i + 1) * MXU]
                for m, _ in enumerate(cols):
                    pltpu.matmul_acc_lhs(accs[turn][m], part, load_staged_rhs=reg)
                if i + 1 < passes:
                    push(ph, cols, i + 1, 1 - reg)
                elif more:
                    push(ph, cols, 0, 1 - reg)
            return seq + passes

        base = (v * ns + s) * rows

        def drain(ph, cols, block, turn):
            place = pl.ds(pl.multiple_of(block * bm, 8), bm)
            for m, c in enumerate(cols):
                lane = slice(c * MXU, (c + 1) * MXU)
                scores = pltpu.matmul_pop(accs[turn][m])
                if ph > 0:
                    scores = scores + acc[place, lane]
                if ph + 1 < len(phases):
                    acc[place, lane] = scores
                    continue
                bent = jnp.tanh(scores * (1.0 / 30.0))
                grown = jnp.exp2(bent * (30.0 * LOG2E))
                want = targets_ref[:, lane] - (base + block * bm)
                index = lax.broadcasted_iota(jnp.int32, (bm, MXU), 0)
                hit = index == want
                if padded > rows:
                    real = index < rows - block * bm
                    hit = hit & real
                    grown = jnp.where(real, grown, 0.0)
                mine = jnp.where(hit, bent, 0.0)
                sums[0:8, lane] += jnp.sum(grown.reshape(bm // 8, 8, MXU), axis=0)
                sums[8:16, lane] += jnp.sum(mine.reshape(bm // 8, 8, MXU), axis=0)

        def phase(ph, cols, events):
            passes = phases[ph][1] // MXU
            trips = max(nblk - 2, 0) // UNROLL
            push(ph, cols, 0, 0)
            feed(ph, cols, 0, 0, 0, nblk > 1)

            def trip(j):
                seq = passes
                for u in range(UNROLL):
                    block = 1 + j * UNROLL + u
                    seq = feed(ph, cols, block, (1 + u) % 2, seq, True)
                    drain(ph, cols, block - 1, u % 2)

            done = 0
            rest = list(range(1 + trips * UNROLL, nblk))
            assert rest or nblk == 1
            for at, action in sorted(events, key=lambda event: event[0]):
                stop = int(at * trips)
                if stop > done:
                    loop(done, stop, trip)
                    done = stop
                action()
            if trips > done:
                loop(done, trips, trip)
            seq = passes * (1 + trips * UNROLL)
            for block in rest:
                seq = feed(ph, cols, block, block % 2, seq, block + 1 < nblk)
                drain(ph, cols, block - 1, (block - 1) % 2)
            drain(ph, cols, nblk - 1, (nblk - 1) % 2)

        for turn in range(2):
            for m in range(2):
                blank = jnp.zeros((bm, MXU), jnp.bfloat16)
                pltpu.matmul_acc_lhs(accs[turn][m], blank, load_staged_rhs=turn)
                pltpu.matmul_pop(accs[turn][m])

        events = [[] for _ in range(planes + 1)]
        for k in range(2, planes):
            events[0].append(((k - 1) / planes, functools.partial(ready, k)))
        for k in range(1, planes):
            when = 0.8 if k == 1 else 0.6
            events[k - 1].append((when, functools.partial(relay, k)))
        for ph in range(len(phases)):
            if ph > 0:
                gathered(ph)
                if ph + 1 < len(phases):
                    fetch(ph + 1)
            fetched(ph)
            for g, cols in enumerate(cols_of):
                phase(ph, cols, events[ph] if g == 0 else [])

    if planes > 1:
        ready(1)
    own_copy.wait()
    gathered(0)
    for i in range(gw // LANES):
        part = slice(i * LANES, (i + 1) * LANES)
        for c in range(tokens // LANES):
            cols = slice(c * LANES, (c + 1) * LANES)
            out = raw[part, cols].astype(jnp.float32) * rbuf[:, cols] * gcol[part, :]
            normed[part, cols] = out.astype(jnp.bfloat16)

    pl.run_scoped(run, *(pltpu.ACC(m)((bm, MXU), jnp.float32)
                         for _ in range(2) for m in range(2)))

    def f_copy(e):
        return remote(fin.at[me], fin.at[me], f_send.at[e], f_recv.at[e], *peer_of(e))

    fin[me, 0:1, :] = jnp.sum(sums[0:8, :], axis=0, keepdims=True)
    fin[me, 1:2, :] = jnp.sum(sums[8:16, :], axis=0, keepdims=True)
    loop(1, count, lambda e: f_copy(count - e).start())
    loop(1, count, lambda e: f_copy(e).wait_recv())
    both = jnp.sum(fin[...], axis=0)
    losses = jnp.log(both[0:1, :]) - 30.0 * both[1:2, :]
    lossbuf[...] = losses
    mean_ref[...] = jnp.sum(losses, axis=1, keepdims=True) / tokens
    loss_ref[...] = lossbuf[:, pl.ds(pl.multiple_of(s * own, LANES), own)]

    loop(1, count, lambda e: s_copy(e).wait_send())
    for k in range(planes):
        if k > 0:
            z_copy(k).wait_send()
        loop(1, half, lambda j: p_copy(k, j).wait_send())
        loop(0, half, lambda j: c_copy(k, j).wait_send())
    loop(1, count, lambda e: f_copy(e).wait_send())


def local(nv, ns, hidden_states, norm_gain, embedding, targets):
    own, width = hidden_states.shape
    rows, features = embedding.shape
    tokens = targets.shape[0]
    group = 2
    while (group * width) % LANES:
        group *= 2
    planes = nv // group
    gw = group * width
    padded = -(-rows // 16) * 16
    bm = block_rows(padded, 400)
    half = (group // 2) * ns
    count = nv * ns
    phases = cut_phases(planes, gw)
    cfg = (nv, ns, group, planes, width, own, tokens, rows, padded, bm, features)
    dma = pltpu.SemaphoreType.DMA
    vmem = pl.BlockSpec(memory_space=pltpu.VMEM)
    loss, mean = pl.pallas_call(
        functools.partial(kernel, cfg),
        out_shape=(jax.ShapeDtypeStruct((1, own), jnp.float32),
                   jax.ShapeDtypeStruct((1, 1), jnp.float32)),
        in_specs=[vmem, vmem, vmem, pl.BlockSpec(memory_space=pl.ANY)],
        out_specs=(vmem, vmem),
        scratch_shapes=[
            pltpu.VMEM((gw, tokens), jnp.bfloat16),
            pltpu.VMEM((max(planes - 1, 1), width, own), jnp.bfloat16),
            pltpu.VMEM((features, tokens), jnp.bfloat16),
            pltpu.VMEM((padded, tokens), jnp.float32),
            pltpu.VMEM((padded, max(n for _, n in phases[0::2])), jnp.bfloat16),
            pltpu.VMEM((padded, max(n for _, n in phases[1::2] or [(0, LANES)])), jnp.bfloat16),
            pltpu.VMEM((features, LANES), jnp.float32),
            pltpu.VMEM((count, 1, own), jnp.float32),
            pltpu.VMEM((1, tokens), jnp.float32),
            pltpu.VMEM((count, 2, tokens), jnp.float32),
            pltpu.VMEM((1, tokens), jnp.float32),
            pltpu.VMEM((16, tokens), jnp.float32),
            dma((planes,)), dma((planes,)),
            dma((planes, half)), dma((planes, half)),
            dma((planes, half)), dma((planes, half)),
            dma((count,)), dma((count,)),
            dma((count,)), dma((count,)),
            dma, dma((len(phases), 2)),
        ],
        compiler_params=pltpu.CompilerParams(
            collective_id=0, has_side_effects=True, vmem_limit_bytes=60 * 2**20),
    )(hidden_states.T, norm_gain.reshape(-1, LANES), targets.reshape(1, -1), embedding)
    return loss.reshape(own), mean.reshape(())


def solution(mesh):
    placed = (P("seq", "vocab"), P(), P(("vocab", "seq"), None), P())
    body = functools.partial(local, mesh.shape["vocab"], mesh.shape["seq"])
    return jax.shard_map(
        body, mesh=mesh, in_specs=placed, out_specs=(P("seq"), P()), check_vma=False
    )
```

time: 69.5 us -> 64.7 us (0.931)
  Pallas kernels: 65.7 us -> 60.9 us
    pallas_call x1, Pallas kernels: 65.7 us -> 60.9 us  [local(): pl.pallas_call(functools.partial(kernel, cfg), out_shape=(jax.ShapeDtypeS...]
where the time goes in v1:
time: 64.7 us; the launch traced here: 64.5 us
  Pallas kernels  60.9 us (94%)
  between operations  2.4 us (4%)
  local copies, waits for them, and re-layouts  1.22 us (2%)
    pallas_call x1, Pallas kernels, local(): pl.pallas_call(functools.partial(kernel, cfg), out_shape=(jax.ShapeDtypeS...  60.9 us

profile of v1, /device:TPU:0, one launch (start us, length us, event | category | flops | bytes accessed | tf_op | source)
XLA Modules:
  0.0 64.5 jit_solution(2444671282921373777)
XLA Ops:
  0.6 60.9 %shard_map.59 = (f32[1,256]{1,0:T(1,128)}, f32[1,1]{1,0:T(1,128)}) custom-call(bf16[224,256]{1,0:T(8,128)(2,1)} %bitcast.5, f32[28,128]{1,0:T(8,128)} %bitcast.6, s32[1,512]{1,0:T(1,128)} %bitcast.7, bf16[8000,3584]{1,0:T(8,128)(2,1)} %emb_ref.1), custom_call_target="tpu_custom_call" | custom-call | tf_op jit(solution)/shard_map/pallas_call | solution.py:335
  61.5 1.2 %copy.8 = f32[256]{0:T(256)} copy(f32[256]{0:T(256)} %bitcast.8) | data formatting | bytes 2048

commit v2 on v1

--- a/solution.py
+++ b/solution.py
@@ -10,6 +10,9 @@
 LANES = 128
 MXU = 256
 UNROLL = 2
+LAG = 2
+READY = (0.0, 0.0, 0.9, 0.34)
+RELAY = (0.0, 0.78, 0.9, 0.78)
 LOG2E = 1.4426950408889634
 
 
@@ -24,9 +27,9 @@
 
 
 def kernel(cfg, ht_ref, gain_ref, targets_ref, emb_ref, loss_ref, mean_ref,
-           raw, zbuf, normed, acc, area_a, area_b, gcol, stat, rbuf, fin, lossbuf,
+           raw, zbuf, normed, acc, area_a, area_b, gcol, chain, stat, rbuf, fin, lossbuf,
            sums, z_send, z_recv, p_send, p_recv, c_send, c_recv, s_send, s_recv,
-           f_send, f_recv, own_sem, e_sem):
+           f_send, f_recv, d_send, d_recv, own_sem, e_sem):
     nv, ns, group, planes, width, own, tokens, rows, padded, bm, features = cfg
     v, s = lax.axis_index("vocab"), lax.axis_index("seq")
     p, q = v // group, v % group
@@ -35,7 +38,9 @@
     hidx = (q // 2) * ns + s
     count = nv * ns
     me = s * nv + v
+    mine_at = s * group + q
     gw = group * width
+    raws = min(2, planes)
     phases = cut_phases(planes, gw)
     nblk = padded // bm
     lanes_of = lambda i: pl.ds(pl.multiple_of(i * LANES, LANES), LANES)
@@ -86,13 +91,32 @@
         pl.semaphore_signal(barrier, inc=1, device_id={"vocab": vv, "seq": ss},
                             device_id_type=pl.DeviceIdType.MESH)
 
-    loop(1, count, greet)
-    fetch(0)
-    if len(phases) > 1:
-        fetch(1)
+    def few(low, high, action):
+        if high - low > 32:
+            loop(low, high, action)
+        else:
+            for i in range(low, high):
+                action(i)
+
+    chain[...] = jnp.zeros_like(chain)
+    few(1, group * ns, greet)
+
+    def call(pp):
+        pl.semaphore_signal(barrier, inc=1, device_id={"vocab": pp * group + q, "seq": s},
+                            device_id_type=pl.DeviceIdType.MESH)
+
+    @pl.when(p > 0)
+    def _():
+        call(p - 1)
+
+    @pl.when(p + 1 < planes)
+    def _():
+        call(p + 1)
+
     h = ht_ref[...].astype(jnp.float32)
-    stat[me] = jnp.sum(h * h, axis=0, keepdims=True)
-    pl.semaphore_wait(barrier, count - 1)
+    chain[2] = jnp.sum(h * h, axis=0, keepdims=True)
+    beside = (p > 0).astype(jnp.int32) + (p + 1 < planes).astype(jnp.int32)
+    pl.semaphore_wait(barrier, group * ns - 1 + beside)
 
     def remote(src, dst, send, recv, vv, ss):
         return pltpu.make_async_remote_copy(
@@ -101,16 +125,39 @@
             device_id_type=pl.DeviceIdType.MESH)
 
     def tile_at(k, qq, ss):
-        place = raw if k == 0 else normed
-        row = 0 if k == 0 else k * gw
+        place = raw if k < raws else normed
+        row = k * gw
         return place.at[pl.ds(pl.multiple_of(row + qq * width, 16), width),
                         pl.ds(pl.multiple_of(ss * own, LANES), own)]
 
     def own_of(k):
         return ht_ref if k == 0 else tile_at(k, q, s)
 
+    def up():
+        return remote(chain.at[3], chain.at[0], d_send.at[0], d_recv.at[0],
+                      (p + 1) * group + q, s)
+
+    def down():
+        return remote(chain.at[4], chain.at[1], d_send.at[1], d_recv.at[1],
+                      (p - 1) * group + q, s)
+
+    def pass_up():
+        chain[3] = chain[2] + chain[0]
+
+        @pl.when(p + 1 < planes)
+        def _():
+            up().start()
+
+    def pass_down():
+        chain[4] = chain[2] + chain[1]
+
+        @pl.when(p > 0)
+        def _():
+            down().start()
+
     def z_copy(k):
-        return remote(ht_ref, zbuf.at[k - 1], z_send.at[k], z_recv.at[k],
+        place = tile_at(k, q, s) if k < raws else zbuf.at[k - raws]
+        return remote(ht_ref, place, z_send.at[k], z_recv.at[k],
                       (p + k) % planes * group + q, s)
 
     def p_copy(k, j):
@@ -129,7 +176,7 @@
                       p * group + (q + 1 - 2 * core), s)
 
     def s_copy(e):
-        return remote(stat.at[me], stat.at[me], s_send.at[e], s_recv.at[e], *peer_of(e))
+        return remote(stat.at[mine_at], stat.at[mine_at], s_send.at[e], s_recv.at[e], *peer_of(e))
 
     def spread(k):
         loop(1, half, lambda j: p_copy(k, j).start())
@@ -144,12 +191,32 @@
     def gathered(k):
         loop(0, half, lambda j: c_copy(k, j).wait_recv())
 
-    loop(1, count, lambda e: s_copy(e).start())
+    @pl.when(p == 0)
+    def _():
+        pass_up()
+
+    @pl.when(p == planes - 1)
+    def _():
+        pass_down()
+
     spread(0)
+    own_copy = pltpu.make_async_copy(ht_ref, tile_at(0, q, s), own_sem)
+    own_copy.start()
+
+    @pl.when(p > 0)
+    def _():
+        up().wait_recv()
+        pass_up()
+
+    @pl.when(p + 1 < planes)
+    def _():
+        down().wait_recv()
+        pass_down()
+
+    stat[mine_at] = chain[0] + chain[1] + chain[2]
+    few(1, group * ns, lambda e: s_copy(e).start())
     for k in range(1, planes):
         z_copy(k).start()
-    own_copy = pltpu.make_async_copy(ht_ref, tile_at(0, q, s), own_sem)
-    own_copy.start()
 
     for k in range(planes):
         for i in range(gw // LANES):
@@ -162,21 +229,34 @@
             area_ref[rows // 16 * 16:, :] = jnp.zeros(
                 (padded - rows // 16 * 16, area_ref.shape[1]), jnp.bfloat16)
 
-    relay(0)
-    loop(1, count, lambda e: s_copy(e).wait_recv())
-    for t in range(ns):
-        meansq = jnp.sum(stat[t * nv:(t + 1) * nv], axis=0) / features
-        rbuf[:, t * own:(t + 1) * own] = lax.rsqrt(meansq + 1e-06)
-
     def ready(k):
         z_copy(k).wait_recv()
         place = tile_at(k, q, s)
-        for c in range(own // LANES):
+        for c in range(own // LANES if k >= raws else 0):
             scale = rbuf[:, lanes_of(s * (own // LANES) + c)]
-            values = zbuf[k - 1, :, c * LANES:(c + 1) * LANES].astype(jnp.float32)
+            values = zbuf[k - raws, :, c * LANES:(c + 1) * LANES].astype(jnp.float32)
             gain = gcol[pl.ds(pl.multiple_of(k * gw + q * width, 16), width), :]
             place[:, c * LANES:(c + 1) * LANES] = (values * scale * gain).astype(jnp.bfloat16)
         spread(k)
+
+    def normalize(k):
+        for i in range(k * gw // LANES, (k + 1) * gw // LANES):
+            part = slice(i * LANES, (i + 1) * LANES)
+            for c in range(tokens // LANES):
+                cols = slice(c * LANES, (c + 1) * LANES)
+                out = raw[part, cols].astype(jnp.float32) * rbuf[:, cols] * gcol[part, :]
+                normed[part, cols] = out.astype(jnp.bfloat16)
+
+    fetch(0)
+    if len(phases) > 1:
+        fetch(1)
+    relay(0)
+    if planes > 1:
+        ready(1)
+    few(1, group * ns, lambda e: s_copy(e).wait_recv())
+    for t in range(ns):
+        meansq = jnp.sum(stat[t * group:(t + 1) * group], axis=0) / features
+        rbuf[:, t * own:(t + 1) * own] = lax.rsqrt(meansq + 1e-06)
 
     def run(*held):
         cols_of = [list(range(c, min(c + 2, tokens // MXU))) for c in range(0, tokens // MXU, 2)]
@@ -212,38 +292,52 @@
                 scores = pltpu.matmul_pop(accs[turn][m])
                 if ph > 0:
                     scores = scores + acc[place, lane]
-                if ph + 1 < len(phases):
-                    acc[place, lane] = scores
-                    continue
-                bent = jnp.tanh(scores * (1.0 / 30.0))
-                grown = jnp.exp2(bent * (30.0 * LOG2E))
-                want = targets_ref[:, lane] - (base + block * bm)
-                index = lax.broadcasted_iota(jnp.int32, (bm, MXU), 0)
-                hit = index == want
-                if padded > rows:
-                    real = index < rows - block * bm
-                    hit = hit & real
-                    grown = jnp.where(real, grown, 0.0)
-                mine = jnp.where(hit, bent, 0.0)
-                sums[0:8, lane] += jnp.sum(grown.reshape(bm // 8, 8, MXU), axis=0)
-                sums[8:16, lane] += jnp.sum(mine.reshape(bm // 8, 8, MXU), axis=0)
+                acc[place, lane] = scores
+
+        def finish(cols, block):
+            for c in cols:
+                lane = slice(c * MXU, (c + 1) * MXU)
+                want = (targets_ref[:, lane] - (base + block * bm)
+                        - lax.broadcasted_iota(jnp.int32, (8, MXU), 0))
+                total, picked = sums[0:8, lane], sums[8:16, lane]
+                for r in range(0, bm, 8):
+                    place = pl.ds(pl.multiple_of(block * bm + r, 8), 8)
+                    bent = jnp.tanh(acc[place, lane] * (1.0 / 30.0))
+                    grown = jnp.exp2(bent * (30.0 * LOG2E))
+                    hit = want == r
+                    if padded > rows:
+                        real = block * bm + r < rows
+                        hit = hit & real
+                        grown = jnp.where(real, grown, 0.0)
+                    picked = jnp.where(hit, bent, picked)
+                    total = total + grown
+                sums[0:8, lane], sums[8:16, lane] = total, picked
 
         def phase(ph, cols, events):
             passes = phases[ph][1] // MXU
-            trips = max(nblk - 2, 0) // UNROLL
+            last = ph + 1 == len(phases)
+            lead = min(LAG if last else 1, nblk)
+            trips = max(nblk - 1 - lead, 0) // UNROLL
+
+            def step(block, turn, seq, more, behind):
+                seq = feed(ph, cols, block, turn, seq, more)
+                if last and behind >= LAG:
+                    finish(cols, block - LAG)
+                if behind > 0:
+                    drain(ph, cols, block - 1, 1 - turn)
+                return seq
+
             push(ph, cols, 0, 0)
-            feed(ph, cols, 0, 0, 0, nblk > 1)
+            seq = 0
+            for block in range(lead):
+                seq = step(block, block % 2, seq, block + 1 < nblk, block)
 
             def trip(j):
-                seq = passes
+                seq = passes * lead
                 for u in range(UNROLL):
-                    block = 1 + j * UNROLL + u
-                    seq = feed(ph, cols, block, (1 + u) % 2, seq, True)
-                    drain(ph, cols, block - 1, u % 2)
+                    seq = step(lead + j * UNROLL + u, (lead + u) % 2, seq, True, lead)
 
             done = 0
-            rest = list(range(1 + trips * UNROLL, nblk))
-            assert rest or nblk == 1
             for at, action in sorted(events, key=lambda event: event[0]):
                 stop = int(at * trips)
                 if stop > done:
@@ -252,11 +346,11 @@
                 action()
             if trips > done:
                 loop(done, trips, trip)
-            seq = passes * (1 + trips * UNROLL)
-            for block in rest:
-                seq = feed(ph, cols, block, block % 2, seq, block + 1 < nblk)
-                drain(ph, cols, block - 1, (block - 1) % 2)
+            for block in range(lead + trips * UNROLL, nblk):
+                seq = step(block, block % 2, passes * block, block + 1 < nblk, block)
             drain(ph, cols, nblk - 1, (nblk - 1) % 2)
+            for block in range(max(nblk - LAG, 0), nblk) if last else ():
+                finish(cols, block)
 
         for turn in range(2):
             for m in range(2):
@@ -266,29 +360,23 @@
 
         events = [[] for _ in range(planes + 1)]
         for k in range(2, planes):
-            events[0].append(((k - 1) / planes, functools.partial(ready, k)))
+            events[max(k - 2, 0)].append((READY[min(k, 3)], functools.partial(ready, k)))
         for k in range(1, planes):
-            when = 0.8 if k == 1 else 0.6
-            events[k - 1].append((when, functools.partial(relay, k)))
+            events[k - 1].append((RELAY[min(k, 3)], functools.partial(relay, k)))
         for ph in range(len(phases)):
             if ph > 0:
                 gathered(ph)
+                if ph < raws:
+                    normalize(ph)
                 if ph + 1 < len(phases):
                     fetch(ph + 1)
             fetched(ph)
             for g, cols in enumerate(cols_of):
                 phase(ph, cols, events[ph] if g == 0 else [])
 
-    if planes > 1:
-        ready(1)
     own_copy.wait()
     gathered(0)
-    for i in range(gw // LANES):
-        part = slice(i * LANES, (i + 1) * LANES)
-        for c in range(tokens // LANES):
-            cols = slice(c * LANES, (c + 1) * LANES)
-            out = raw[part, cols].astype(jnp.float32) * rbuf[:, cols] * gcol[part, :]
-            normed[part, cols] = out.astype(jnp.bfloat16)
+    normalize(0)
 
     pl.run_scoped(run, *(pltpu.ACC(m)((bm, MXU), jnp.float32)
                          for _ in range(2) for m in range(2)))
@@ -298,21 +386,28 @@
 
     fin[me, 0:1, :] = jnp.sum(sums[0:8, :], axis=0, keepdims=True)
     fin[me, 1:2, :] = jnp.sum(sums[8:16, :], axis=0, keepdims=True)
-    loop(1, count, lambda e: f_copy(count - e).start())
+    few(1, count, lambda e: f_copy(count - e).start())
+    loop(1, group * ns, lambda e: s_copy(e).wait_send())
+    @pl.when(p + 1 < planes)
+    def _():
+        up().wait_send()
+
+    @pl.when(p > 0)
+    def _():
+        down().wait_send()
+
+    for k in range(planes):
+        if k > 0:
+            z_copy(k).wait_send()
+        loop(1, half, lambda j: p_copy(k, j).wait_send())
+        loop(0, half, lambda j: c_copy(k, j).wait_send())
+    loop(1, count, lambda e: f_copy(e).wait_send())
     loop(1, count, lambda e: f_copy(e).wait_recv())
     both = jnp.sum(fin[...], axis=0)
     losses = jnp.log(both[0:1, :]) - 30.0 * both[1:2, :]
     lossbuf[...] = losses
     mean_ref[...] = jnp.sum(losses, axis=1, keepdims=True) / tokens
     loss_ref[...] = lossbuf[:, pl.ds(pl.multiple_of(s * own, LANES), own)]
-
-    loop(1, count, lambda e: s_copy(e).wait_send())
-    for k in range(planes):
-        if k > 0:
-            z_copy(k).wait_send()
-        loop(1, half, lambda j: p_copy(k, j).wait_send())
-        loop(0, half, lambda j: c_copy(k, j).wait_send())
-    loop(1, count, lambda e: f_copy(e).wait_send())
 
 
 def local(nv, ns, hidden_states, norm_gain, embedding, targets):
@@ -334,19 +429,19 @@
     vmem = pl.BlockSpec(memory_space=pltpu.VMEM)
     loss, mean = pl.pallas_call(
         functools.partial(kernel, cfg),
-        out_shape=(jax.ShapeDtypeStruct((1, own), jnp.float32),
-                   jax.ShapeDtypeStruct((1, 1), jnp.float32)),
+        out_shape=(pltpu.VMEM((1, own), jnp.float32), pltpu.VMEM((1, 1), jnp.float32)),
         in_specs=[vmem, vmem, vmem, pl.BlockSpec(memory_space=pl.ANY)],
         out_specs=(vmem, vmem),
         scratch_shapes=[
-            pltpu.VMEM((gw, tokens), jnp.bfloat16),
-            pltpu.VMEM((max(planes - 1, 1), width, own), jnp.bfloat16),
+            pltpu.VMEM((min(2, planes) * gw, tokens), jnp.bfloat16),
+            pltpu.VMEM((max(planes - 2, 1), width, own), jnp.bfloat16),
             pltpu.VMEM((features, tokens), jnp.bfloat16),
             pltpu.VMEM((padded, tokens), jnp.float32),
             pltpu.VMEM((padded, max(n for _, n in phases[0::2])), jnp.bfloat16),
             pltpu.VMEM((padded, max(n for _, n in phases[1::2] or [(0, LANES)])), jnp.bfloat16),
             pltpu.VMEM((features, LANES), jnp.float32),
-            pltpu.VMEM((count, 1, own), jnp.float32),
+            pltpu.VMEM((5, 1, own), jnp.float32),
+            pltpu.VMEM((group * ns, 1, own), jnp.float32),
             pltpu.VMEM((1, tokens), jnp.float32),
             pltpu.VMEM((count, 2, tokens), jnp.float32),
             pltpu.VMEM((1, tokens), jnp.float32),
@@ -354,8 +449,9 @@
             dma((planes,)), dma((planes,)),
             dma((planes, half)), dma((planes, half)),
             dma((planes, half)), dma((planes, half)),
+            dma((group * ns,)), dma((group * ns,)),
             dma((count,)), dma((count,)),
-            dma((count,)), dma((count,)),
+            dma((2,)), dma((2,)),
             dma, dma((len(phases), 2)),
         ],
         compiler_params=pltpu.CompilerParams(

time: 64.7 us -> 63.4 us (0.980)
  local copies, waits for them, and re-layouts: 1.22 us -> 0.56 us
    unnamed x1, local copies, waits for them, and re-layouts: 1.22 us -> 0.56 us
where the time goes in v2:
time: 63.4 us; the launch traced here: 63.3 us
  Pallas kernels  60.9 us (96%)
  between operations  1.8 us (3%)
    pallas_call x1, Pallas kernels, local(): pl.pallas_call(functools.partial(kernel, cfg), out_shape=(pltpu.VMEM((1,...  60.9 us

profile of v2, /device:TPU:0, one launch (start us, length us, event | category | flops | bytes accessed | tf_op | source)
XLA Modules:
  0.0 63.3 jit_solution(18279561888155345275)
XLA Ops:
  0.6 60.9 %shard_map.59 = (f32[1,256]{1,0:T(1,128)S(1)}, f32[1,1]{1,0:T(1,128)S(1)}) custom-call(bf16[224,256]{1,0:T(8,128)(2,1)} %bitcast.6, f32[28,128]{1,0:T(8,128)} %bitcast.7, s32[1,512]{1,0:T(1,128)} %bitcast.8, bf16[8000,3584]{1,0:T(8,128)(2,1)} %emb_ref.1), custom_call_target="tpu_custom_call" | custom-call | tf_op jit(solution)/shard_map/pallas_call | solution.py:430
  61.6 0.6 copy.8

commit v3 on v2

--- a/solution.py
+++ b/solution.py
@@ -10,6 +10,7 @@
 LANES = 128
 MXU = 256
 UNROLL = 2
+LAST_UNROLL = 8
 LAG = 2
 READY = (0.0, 0.0, 0.9, 0.34)
 RELAY = (0.0, 0.78, 0.9, 0.78)
@@ -113,6 +114,9 @@
     def _():
         call(p + 1)
 
+    fetch(0)
+    if len(phases) > 1:
+        fetch(1)
     h = ht_ref[...].astype(jnp.float32)
     chain[2] = jnp.sum(h * h, axis=0, keepdims=True)
     beside = (p > 0).astype(jnp.int32) + (p + 1 < planes).astype(jnp.int32)
@@ -208,6 +212,11 @@
         up().wait_recv()
         pass_up()
 
+    if planes > 1:
+        @pl.when(p + 1 < planes)
+        def _():
+            z_copy(1).start()
+
     @pl.when(p + 1 < planes)
     def _():
         down().wait_recv()
@@ -215,7 +224,12 @@
 
     stat[mine_at] = chain[0] + chain[1] + chain[2]
     few(1, group * ns, lambda e: s_copy(e).start())
-    for k in range(1, planes):
+    if planes > 1:
+        @pl.when(p + 1 == planes)
+        def _():
+            z_copy(1).start()
+
+    for k in range(2, planes):
         z_copy(k).start()
 
     for k in range(planes):
@@ -247,9 +261,6 @@
                 out = raw[part, cols].astype(jnp.float32) * rbuf[:, cols] * gcol[part, :]
                 normed[part, cols] = out.astype(jnp.bfloat16)
 
-    fetch(0)
-    if len(phases) > 1:
-        fetch(1)
     relay(0)
     if planes > 1:
         ready(1)
@@ -317,7 +328,8 @@
             passes = phases[ph][1] // MXU
             last = ph + 1 == len(phases)
             lead = min(LAG if last else 1, nblk)
-            trips = max(nblk - 1 - lead, 0) // UNROLL
+            unroll = LAST_UNROLL if last else UNROLL
+            trips = max(nblk - 1 - lead, 0) // unroll
 
             def step(block, turn, seq, more, behind):
                 seq = feed(ph, cols, block, turn, seq, more)
@@ -334,8 +346,8 @@
 
             def trip(j):
                 seq = passes * lead
-                for u in range(UNROLL):
-                    seq = step(lead + j * UNROLL + u, (lead + u) % 2, seq, True, lead)
+                for u in range(unroll):
+                    seq = step(lead + j * unroll + u, (lead + u) % 2, seq, True, lead)
 
             done = 0
             for at, action in sorted(events, key=lambda event: event[0]):
@@ -346,7 +358,7 @@
                 action()
             if trips > done:
                 loop(done, trips, trip)
-            for block in range(lead + trips * UNROLL, nblk):
+            for block in range(lead + trips * unroll, nblk):
                 seq = step(block, block % 2, passes * block, block + 1 < nblk, block)
             drain(ph, cols, nblk - 1, (nblk - 1) % 2)
             for block in range(max(nblk - LAG, 0), nblk) if last else ():

time: 63.4 us -> 60 us (0.946)
  Pallas kernels: 60.9 us -> 57.5 us
    pallas_call x1, Pallas kernels: 60.9 us -> 57.5 us  [local(): pl.pallas_call(functools.partial(kernel, cfg), out_shape=(pltpu.VMEM((1,...]
where the time goes in v3:
time: 60 us; the launch traced here: 59.9 us
  Pallas kernels  57.5 us (96%)
  between operations  1.8 us (3%)
    pallas_call x1, Pallas kernels, local(): pl.pallas_call(functools.partial(kernel, cfg), out_shape=(pltpu.VMEM((1,...  57.5 us

profile of v3, /device:TPU:0, one launch (start us, length us, event | category | flops | bytes accessed | tf_op | source)
XLA Modules:
  0.0 59.9 jit_solution(14816525736492902959)
XLA Ops:
  0.6 57.5 %shard_map.59 = (f32[1,256]{1,0:T(1,128)S(1)}, f32[1,1]{1,0:T(1,128)S(1)}) custom-call(bf16[224,256]{1,0:T(8,128)(2,1)} %bitcast.6, f32[28,128]{1,0:T(8,128)} %bitcast.7, s32[1,512]{1,0:T(1,128)} %bitcast.8, bf16[8000,3584]{1,0:T(8,128)(2,1)} %emb_ref.1), custom_call_target="tpu_custom_call" | custom-call | tf_op jit(solution)/shard_map/pallas_call | solution.py:442
  58.2 0.6 copy.8

commit v4 on v3

--- a/solution.py
+++ b/solution.py
@@ -166,17 +166,17 @@
 
     def p_copy(k, j):
         other = (hidx + j) % half
-        return remote(own_of(k), tile_at(k, q, s), p_send.at[k, j], p_recv.at[k, j],
+        return remote(own_of(k), tile_at(k, q, s), (p_send.at[k, j] if k == 0 else z_send.at[k]), p_recv.at[k, j],
                       p * group + 2 * (other // ns) + core, other % ns)
 
     def c_copy(k, j):
         tile = (hidx + half - j) % half
         place = tile_at(k, 2 * (tile // ns) + core, tile % ns)
-        return remote(place, place, c_send.at[k, j], c_recv.at[k, j],
+        return remote(place, place, (c_send.at[k, j] if k == 0 else z_send.at[k]), c_recv.at[k, j],
                       p * group + (q + 1 - 2 * core), s)
 
     def c_own(k):
-        return remote(own_of(k), tile_at(k, q, s), c_send.at[k, 0], c_recv.at[k, 0],
+        return remote(own_of(k), tile_at(k, q, s), (c_send.at[k, 0] if k == 0 else z_send.at[k]), c_recv.at[k, 0],
                       p * group + (q + 1 - 2 * core), s)
 
     def s_copy(e):
@@ -394,7 +394,7 @@
                          for _ in range(2) for m in range(2)))
 
     def f_copy(e):
-        return remote(fin.at[me], fin.at[me], f_send.at[e], f_recv.at[e], *peer_of(e))
+        return remote(fin.at[me], fin.at[me], f_send, f_recv, *peer_of(e))
 
     fin[me, 0:1, :] = jnp.sum(sums[0:8, :], axis=0, keepdims=True)
     fin[me, 1:2, :] = jnp.sum(sums[8:16, :], axis=0, keepdims=True)
@@ -408,13 +408,15 @@
     def _():
         down().wait_send()
 
-    for k in range(planes):
-        if k > 0:
-            z_copy(k).wait_send()
-        loop(1, half, lambda j: p_copy(k, j).wait_send())
-        loop(0, half, lambda j: c_copy(k, j).wait_send())
-    loop(1, count, lambda e: f_copy(e).wait_send())
-    loop(1, count, lambda e: f_copy(e).wait_recv())
+    loop(1, half, lambda j: p_copy(0, j).wait_send())
+    loop(0, half, lambda j: c_copy(0, j).wait_send())
+    for k in range(1, planes):
+        whole = (raw if k < raws else normed).at[k * gw:(k + 1) * gw, :]
+        remote(whole, whole, z_send.at[k], z_recv.at[k], *peer_of(1)).wait_send()
+    others = fin.at[0:count - 1]
+    shared = remote(others, others, f_send, f_recv, *peer_of(1))
+    shared.wait_send()
+    shared.wait_recv()
     both = jnp.sum(fin[...], axis=0)
     losses = jnp.log(both[0:1, :]) - 30.0 * both[1:2, :]
     lossbuf[...] = losses
@@ -462,7 +464,7 @@
             dma((planes, half)), dma((planes, half)),
             dma((planes, half)), dma((planes, half)),
             dma((group * ns,)), dma((group * ns,)),
-            dma((count,)), dma((count,)),
+            dma, dma,
             dma((2,)), dma((2,)),
             dma, dma((len(phases), 2)),
         ],

time: 60 us -> 59.3 us (0.988)
  Pallas kernels: 57.5 us -> 56.8 us
    pallas_call x1, Pallas kernels: 57.5 us -> 56.8 us  [local(): pl.pallas_call(functools.partial(kernel, cfg), out_shape=(pltpu.VMEM((1,...]
where the time goes in v4:
time: 59.3 us; the launch traced here: 59.2 us
  Pallas kernels  56.8 us (96%)
  between operations  1.8 us (3%)
    pallas_call x1, Pallas kernels, local(): pl.pallas_call(functools.partial(kernel, cfg), out_shape=(pltpu.VMEM((1,...  56.8 us

profile of v4, /device:TPU:0, one launch (start us, length us, event | category | flops | bytes accessed | tf_op | source)
XLA Modules:
  0.0 59.2 jit_solution(18175470132492852894)
XLA Ops:
  0.6 56.8 %shard_map.59 = (f32[1,256]{1,0:T(1,128)S(1)}, f32[1,1]{1,0:T(1,128)S(1)}) custom-call(bf16[224,256]{1,0:T(8,128)(2,1)} %bitcast.6, f32[28,128]{1,0:T(8,128)} %bitcast.7, s32[1,512]{1,0:T(1,128)} %bitcast.8, bf16[8000,3584]{1,0:T(8,128)(2,1)} %emb_ref.1), custom_call_target="tpu_custom_call" | custom-call | tf_op jit(solution)/shard_map/pallas_call | solution.py:444
  57.5 0.6 copy.8
